TPU v7x, 32 devices: a whole 2x2x4 slice. The times are simulated.
32 devices in a mesh: groups: 2 (over x), seq: 16 (over z, y, core).
Axes of the slice: x: 2, y: 2, z: 4, core: 2. Of those that a mesh axis runs over, the one named last changes fastest.
Arguments:
- candidates: bfloat16 [32, 256, 256], P('groups', 'seq'), parts along dimension 0, may hold values from -110 to 110
- codes: int32 [32, 2048, 256], P('groups', 'seq'), parts along dimension 0, may hold values from -2147483648 to 2147483647
- scale_index: int32 [32, 8192], P('groups', 'seq'), parts along dimension 0, may hold values from 0 to 255
- lengths: int32 [32], P('groups'), parts along dimension 0, may hold values from 128 to 8192, as said below
- scale_table: float32 [256], replicated, may hold values from 0.004 to 0.04
- query_weight: bfloat16 [256, 256], replicated, may hold values from -0.375 to 0.375
- key_weight: bfloat16 [256, 256], replicated, may hold values from -0.375 to 0.375
- value_weight: bfloat16 [256, 256], replicated, may hold values from -0.375 to 0.375
- out_weight: bfloat16 [256, 256], replicated, may hold values from -0.375 to 0.375
- norm_gain: float32 [256], replicated, may hold values from 0.1 to 1.9
- hidden_weight: bfloat16 [256, 512], replicated, may hold values from -0.375 to 0.375
- hidden_bias: float32 [512], replicated, may hold values from -4 to 4
- score_weight: bfloat16 [512], replicated, may hold values from -0.25 to 0.25
Outputs:
- interest: bfloat16 [32, 256, 256], P('groups', 'seq'), parts along dimension 0
- logits: float32 [32, 256], P('groups', 'seq'), parts along dimension 0
There are 2 independent parts, one for each index of `groups`. A program takes and returns all parts, laid end to end along the dimension named above; an argument that names none is the same for every part. Nothing has to cross between parts.
Inputs may be any that keep to these rules, and one draw needn't show every extreme that they name: `lengths`: each user's history length is a multiple of 128; in every draw some user's length is 8192.
All inputs are finite; a program needn't handle non-finite values.
Results may differ from a plain program's by a relative error of at most 0.02.
The roundings to bfloat16 on the way count: a program that leaves them out, or rounds other values in their place, can miss the bound.
Values may be sent and summed in bfloat16 or wider, within the bound.
A program may use at most 128 MiB of HBM per device.

v0:
```python
import math

import jax
import jax.numpy as jnp
from jax import lax
from jax.sharding import PartitionSpec as P

HEADS = 4


NEG_FILL = -1e30


def unpack_codes(words):
    byte_rows = [jnp.right_shift(jnp.left_shift(words, 24 - 8 * k), 24) for k in range(4)]
    stacked = jnp.stack(byte_rows, axis=1)
    return stacked.reshape(words.shape[0] * 4, words.shape[1])


def score_block(query_rows, key_rows, live_row):
    cand_rows, model_width = query_rows.shape
    head_size = model_width // HEADS
    split_query = query_rows.reshape(cand_rows, HEADS, head_size)
    split_keys = key_rows.reshape(key_rows.shape[0], HEADS, head_size)
    scores = jnp.einsum("chd,khd->hck", split_query, split_keys, preferred_element_type=jnp.float32)
    scores = scores * (1.0 / math.sqrt(head_size))
    return jnp.where(live_row[None, None, :], scores, NEG_FILL)


def exp_weights(scores, live_row, peak_rows):
    return jnp.where(live_row[None, None, :], jnp.exp(scores - peak_rows[:, :, None]), 0.0)


def weighted_rows(weights, value_rows):
    head_count, cand_rows, key_count = weights.shape
    split_values = value_rows.reshape(key_count, head_count, -1)
    blended = jnp.einsum(
        "hck,khd->chd",
        weights.astype(jnp.bfloat16),
        split_values,
        preferred_element_type=jnp.float32,
    )
    return blended.reshape(cand_rows, -1)


def local_partials(user_item):
    query_rows, key_rows, value_rows, live_row = user_item
    scores = score_block(query_rows, key_rows, live_row)
    peak_rows = jnp.max(scores, axis=2)
    weights = exp_weights(scores, live_row, peak_rows)
    return (weighted_rows(weights, value_rows), jnp.sum(weights, axis=2), peak_rows)


def on_device(
    candidates,
    codes,
    scale_index,
    lengths,
    scale_table,
    query_weight,
    key_weight,
    value_weight,
    out_weight,
    norm_gain,
    hidden_weight,
    hidden_bias,
    score_weight,
):
    user_count, cand_local, model_width = candidates.shape
    hist_local = scale_index.shape[1]
    head_size = model_width // HEADS
    own_queries = jnp.einsum(
        "ucd,de->uce", candidates, query_weight, preferred_element_type=jnp.float32
    ).astype(jnp.bfloat16)
    queries = lax.all_gather(own_queries, "seq", axis=1, tiled=True)
    offset = lax.axis_index("seq") * hist_local
    places = offset + jnp.arange(hist_local, dtype=jnp.int32)
    live_mask = places[None, :] < lengths[:, None]
    levels = jnp.arange(scale_table.shape[0], dtype=jnp.int32)

    def project(user_item):
        word_rows, index_rows = user_item
        code_rows = unpack_codes(word_rows)
        row_scales = jnp.sum(
            jnp.where(index_rows[:, None] == levels[None, :], scale_table[None, :], 0.0), axis=1
        )
        history = (code_rows.astype(jnp.float32) * row_scales[:, None]).astype(jnp.bfloat16)
        key_rows = jnp.dot(history, key_weight, preferred_element_type=jnp.float32).astype(
            jnp.bfloat16
        )
        value_rows = jnp.dot(history, value_weight, preferred_element_type=jnp.float32).astype(
            jnp.bfloat16
        )
        return (key_rows, value_rows)

    all_keys, all_values = lax.map(project, (codes, scale_index))
    numerators, totals, peak_rows = lax.map(
        local_partials, (queries, all_keys, all_values, live_mask)
    )
    got_numerators = lax.all_to_all(
        numerators[None].astype(jnp.bfloat16), "seq", split_axis=2, concat_axis=0, tiled=True
    ).astype(jnp.float32)
    got_peaks, got_totals = (
        lax.all_to_all(peak_rows[None], "seq", split_axis=3, concat_axis=0, tiled=True),
        lax.all_to_all(totals[None], "seq", split_axis=3, concat_axis=0, tiled=True),
    )
    global_peaks = jnp.max(got_peaks, axis=0)
    factor = jnp.exp(got_peaks - global_peaks[None])
    totals = jnp.sum(factor * got_totals, axis=0)
    sources = got_numerators.shape[0]
    scaled = (
        got_numerators.reshape(sources, user_count, cand_local, HEADS, head_size)
        * jnp.transpose(factor, (0, 1, 3, 2))[..., None]
    )
    numerators = jnp.sum(scaled, axis=0).reshape(user_count, cand_local, model_width)
    split_numer = numerators.reshape(user_count, cand_local, HEADS, head_size)
    attended = (
        (split_numer / jnp.transpose(totals, (0, 2, 1))[..., None])
        .reshape(user_count, cand_local, model_width)
        .astype(jnp.bfloat16)
    )
    interest = jnp.einsum(
        "ucd,de->uce", attended, out_weight, preferred_element_type=jnp.float32
    ).astype(jnp.bfloat16)
    floats = interest.astype(jnp.float32)
    normed = (
        floats * lax.rsqrt(jnp.mean(floats * floats, axis=2, keepdims=True) + 1e-06) * norm_gain
    ).astype(jnp.bfloat16)
    hidden = jax.nn.silu(
        jnp.einsum("ucd,dh->uch", normed, hidden_weight, preferred_element_type=jnp.float32)
        + hidden_bias
    ).astype(jnp.bfloat16)
    logits = jnp.einsum("uch,h->uc", hidden, score_weight, preferred_element_type=jnp.float32)
    return (interest, logits)


def solution(mesh):
    placed = (
        P("groups", "seq", None),
        P("groups", "seq", None),
        P("groups", "seq"),
        P("groups"),
        P(),
        P(),
        P(),
        P(),
        P(),
        P(),
        P(),
        P(),
        P(),
    )
    return jax.shard_map(
        on_device,
        mesh=mesh,
        in_specs=placed,
        out_specs=(P("groups", "seq", None), P("groups", "seq")),
        check_vma=False,
    )
```

profile of v0, /device:TPU:13, one launch (start us, length us, event | category | flops | bytes accessed | tf_op | source)
XLA Modules:
  0.0 369.4 jit_solution(11931711030557221657)
XLA Ops:
  7.2 1.8 convolution_convert_fusion.3
  9.1 80.3 %while.28 = (s32[]{:T(128)}, bf16[16,512,256]{2,1,0:T(8,128)(2,1)}, bf16[16,512,256]{2,1,0:T(8,128)(2,1)}, s32[16,128,256]{2,1,0:T(8,128)}, s32[16,512]{1,0:T(8,...) while((s32[]{:T(128)}, bf16[16,512,256]{2,1,0:T(8,128)(2,1)}, ...), condition=%wide.region_2.3_spmd.clone, body=%wide.region_0.2_spmd.clone.sunk | while | flops 136183296 | bytes 5916857 | solution.py:96
  22.2 1.0 fusion.65
  27.2 1.0 fusion.65
  28.2 1.0 fusion.64
  32.2 1.0 fusion.65
  33.2 1.0 fusion.64
  37.2 1.0 fusion.65
  38.2 1.0 fusion.64
  42.3 1.0 fusion.65
  47.3 1.0 fusion.65
  48.3 1.0 fusion.64
  49.3 1.0 constant_dynamic-slice_fusion.13
  52.3 1.0 fusion.65
  53.3 1.0 fusion.64
  62.4 1.0 fusion.65
  67.4 1.0 fusion.65
  68.4 1.0 fusion.64
  73.4 1.0 fusion.64
  87.4 1.0 fusion.65
  89.5 191.5 %while.27 = (s32[]{:T(128)}, bf16[16,256,256]{2,0,1:T(8,128)(2,1)}, f32[16,4,256]{2,1,0:T(4,128)S(1)}, f32[16,4,256]{2,1,0:T(4,128)S(1)}, bf16[16,512,256]{2,1,0...) while((s32[]{:T(128)}, bf16[16,256,256]{2,0,1:T(8,128)(2,1)}, ...), condition=%wide.region_6.7_spmd, body=%wide.region_3.6_spmd.sunk | while | flops 141031424 | bytes 10259069 | solution.py:97
  94.8 6.6 %dynamic_update_slice.29 = bf16[16,256,256]{2,0,1:T(8,128)(2,1)} dynamic-update-slice(bf16[16,256,256]{2,0,1:T(8,128)(2,1)} %get-tuple-element.385, bf16[1,256,256]{2,0,1:T(2,128)(2,1)S(1)} %copy.82, s32[]{:T(128)} %get-tuple-element.384, s32[]{:T(128)} %constant.40.clone.1..sunk, s32[]{:T(128)} %constant.40.clone.1..sunk) | dynamic-update-slice | bytes 262148 | tf_op jit(solution)/shard_map/while/body/jit(dynamic_update_index_in_dim)/dynamic_update_slice | solution.py:97
  106.8 6.6 %dynamic_update_slice.29 = bf16[16,256,256]{2,0,1:T(8,128)(2,1)} dynamic-update-slice(bf16[16,256,256]{2,0,1:T(8,128)(2,1)} %get-tuple-element.385, bf16[1,256,256]{2,0,1:T(2,128)(2,1)S(1)} %copy.82, s32[]{:T(128)} %get-tuple-element.384, s32[]{:T(128)} %constant.40.clone.1..sunk, s32[]{:T(128)} %constant.40.clone.1..sunk) | dynamic-update-slice | bytes 262148 | tf_op jit(solution)/shard_map/while/body/jit(dynamic_update_index_in_dim)/dynamic_update_slice | solution.py:97
  118.8 6.6 %dynamic_update_slice.29 = bf16[16,256,256]{2,0,1:T(8,128)(2,1)} dynamic-update-slice(bf16[16,256,256]{2,0,1:T(8,128)(2,1)} %get-tuple-element.385, bf16[1,256,256]{2,0,1:T(2,128)(2,1)S(1)} %copy.82, s32[]{:T(128)} %get-tuple-element.384, s32[]{:T(128)} %constant.40.clone.1..sunk, s32[]{:T(128)} %constant.40.clone.1..sunk) | dynamic-update-slice | bytes 262148 | tf_op jit(solution)/shard_map/while/body/jit(dynamic_update_index_in_dim)/dynamic_update_slice | solution.py:97
  130.8 6.6 %dynamic_update_slice.29 = bf16[16,256,256]{2,0,1:T(8,128)(2,1)} dynamic-update-slice(bf16[16,256,256]{2,0,1:T(8,128)(2,1)} %get-tuple-element.385, bf16[1,256,256]{2,0,1:T(2,128)(2,1)S(1)} %copy.82, s32[]{:T(128)} %get-tuple-element.384, s32[]{:T(128)} %constant.40.clone.1..sunk, s32[]{:T(128)} %constant.40.clone.1..sunk) | dynamic-update-slice | bytes 262148 | tf_op jit(solution)/shard_map/while/body/jit(dynamic_update_index_in_dim)/dynamic_update_slice | solution.py:97
  142.7 6.6 %dynamic_update_slice.29 = bf16[16,256,256]{2,0,1:T(8,128)(2,1)} dynamic-update-slice(bf16[16,256,256]{2,0,1:T(8,128)(2,1)} %get-tuple-element.385, bf16[1,256,256]{2,0,1:T(2,128)(2,1)S(1)} %copy.82, s32[]{:T(128)} %get-tuple-element.384, s32[]{:T(128)} %constant.40.clone.1..sunk, s32[]{:T(128)} %constant.40.clone.1..sunk) | dynamic-update-slice | bytes 262148 | tf_op jit(solution)/shard_map/while/body/jit(dynamic_update_index_in_dim)/dynamic_update_slice | solution.py:97
  154.7 6.6 %dynamic_update_slice.29 = bf16[16,256,256]{2,0,1:T(8,128)(2,1)} dynamic-update-slice(bf16[16,256,256]{2,0,1:T(8,128)(2,1)} %get-tuple-element.385, bf16[1,256,256]{2,0,1:T(2,128)(2,1)S(1)} %copy.82, s32[]{:T(128)} %get-tuple-element.384, s32[]{:T(128)} %constant.40.clone.1..sunk, s32[]{:T(128)} %constant.40.clone.1..sunk) | dynamic-update-slice | bytes 262148 | tf_op jit(solution)/shard_map/while/body/jit(dynamic_update_index_in_dim)/dynamic_update_slice | solution.py:97
  166.7 6.6 %dynamic_update_slice.29 = bf16[16,256,256]{2,0,1:T(8,128)(2,1)} dynamic-update-slice(bf16[16,256,256]{2,0,1:T(8,128)(2,1)} %get-tuple-element.385, bf16[1,256,256]{2,0,1:T(2,128)(2,1)S(1)} %copy.82, s32[]{:T(128)} %get-tuple-element.384, s32[]{:T(128)} %constant.40.clone.1..sunk, s32[]{:T(128)} %constant.40.clone.1..sunk) | dynamic-update-slice | bytes 262148 | tf_op jit(solution)/shard_map/while/body/jit(dynamic_update_index_in_dim)/dynamic_update_slice | solution.py:97
  178.7 6.6 %dynamic_update_slice.29 = bf16[16,256,256]{2,0,1:T(8,128)(2,1)} dynamic-update-slice(bf16[16,256,256]{2,0,1:T(8,128)(2,1)} %get-tuple-element.385, bf16[1,256,256]{2,0,1:T(2,128)(2,1)S(1)} %copy.82, s32[]{:T(128)} %get-tuple-element.384, s32[]{:T(128)} %constant.40.clone.1..sunk, s32[]{:T(128)} %constant.40.clone.1..sunk) | dynamic-update-slice | bytes 262148 | tf_op jit(solution)/shard_map/while/body/jit(dynamic_update_index_in_dim)/dynamic_update_slice | solution.py:97
  190.6 6.6 %dynamic_update_slice.29 = bf16[16,256,256]{2,0,1:T(8,128)(2,1)} dynamic-update-slice(bf16[16,256,256]{2,0,1:T(8,128)(2,1)} %get-tuple-element.385, bf16[1,256,256]{2,0,1:T(2,128)(2,1)S(1)} %copy.82, s32[]{:T(128)} %get-tuple-element.384, s32[]{:T(128)} %constant.40.clone.1..sunk, s32[]{:T(128)} %constant.40.clone.1..sunk) | dynamic-update-slice | bytes 262148 | tf_op jit(solution)/shard_map/while/body/jit(dynamic_update_index_in_dim)/dynamic_update_slice | solution.py:97
  202.6 6.6 %dynamic_update_slice.29 = bf16[16,256,256]{2,0,1:T(8,128)(2,1)} dynamic-update-slice(bf16[16,256,256]{2,0,1:T(8,128)(2,1)} %get-tuple-element.385, bf16[1,256,256]{2,0,1:T(2,128)(2,1)S(1)} %copy.82, s32[]{:T(128)} %get-tuple-element.384, s32[]{:T(128)} %constant.40.clone.1..sunk, s32[]{:T(128)} %constant.40.clone.1..sunk) | dynamic-update-slice | bytes 262148 | tf_op jit(solution)/shard_map/while/body/jit(dynamic_update_index_in_dim)/dynamic_update_slice | solution.py:97
  214.6 6.6 %dynamic_update_slice.29 = bf16[16,256,256]{2,0,1:T(8,128)(2,1)} dynamic-update-slice(bf16[16,256,256]{2,0,1:T(8,128)(2,1)} %get-tuple-element.385, bf16[1,256,256]{2,0,1:T(2,128)(2,1)S(1)} %copy.82, s32[]{:T(128)} %get-tuple-element.384, s32[]{:T(128)} %constant.40.clone.1..sunk, s32[]{:T(128)} %constant.40.clone.1..sunk) | dynamic-update-slice | bytes 262148 | tf_op jit(solution)/shard_map/while/body/jit(dynamic_update_index_in_dim)/dynamic_update_slice | solution.py:97
  226.5 6.6 %dynamic_update_slice.29 = bf16[16,256,256]{2,0,1:T(8,128)(2,1)} dynamic-update-slice(bf16[16,256,256]{2,0,1:T(8,128)(2,1)} %get-tuple-element.385, bf16[1,256,256]{2,0,1:T(2,128)(2,1)S(1)} %copy.82, s32[]{:T(128)} %get-tuple-element.384, s32[]{:T(128)} %constant.40.clone.1..sunk, s32[]{:T(128)} %constant.40.clone.1..sunk) | dynamic-update-slice | bytes 262148 | tf_op jit(solution)/shard_map/while/body/jit(dynamic_update_index_in_dim)/dynamic_update_slice | solution.py:97
  238.5 6.6 %dynamic_update_slice.29 = bf16[16,256,256]{2,0,1:T(8,128)(2,1)} dynamic-update-slice(bf16[16,256,256]{2,0,1:T(8,128)(2,1)} %get-tuple-element.385, bf16[1,256,256]{2,0,1:T(2,128)(2,1)S(1)} %copy.82, s32[]{:T(128)} %get-tuple-element.384, s32[]{:T(128)} %constant.40.clone.1..sunk, s32[]{:T(128)} %constant.40.clone.1..sunk) | dynamic-update-slice | bytes 262148 | tf_op jit(solution)/shard_map/while/body/jit(dynamic_update_index_in_dim)/dynamic_update_slice | solution.py:97
  250.5 6.6 %dynamic_update_slice.29 = bf16[16,256,256]{2,0,1:T(8,128)(2,1)} dynamic-update-slice(bf16[16,256,256]{2,0,1:T(8,128)(2,1)} %get-tuple-element.385, bf16[1,256,256]{2,0,1:T(2,128)(2,1)S(1)} %copy.82, s32[]{:T(128)} %get-tuple-element.384, s32[]{:T(128)} %constant.40.clone.1..sunk, s32[]{:T(128)} %constant.40.clone.1..sunk) | dynamic-update-slice | bytes 262148 | tf_op jit(solution)/shard_map/while/body/jit(dynamic_update_index_in_dim)/dynamic_update_slice | solution.py:97
  262.4 6.6 %dynamic_update_slice.29 = bf16[16,256,256]{2,0,1:T(8,128)(2,1)} dynamic-update-slice(bf16[16,256,256]{2,0,1:T(8,128)(2,1)} %get-tuple-element.385, bf16[1,256,256]{2,0,1:T(2,128)(2,1)S(1)} %copy.82, s32[]{:T(128)} %get-tuple-element.384, s32[]{:T(128)} %constant.40.clone.1..sunk, s32[]{:T(128)} %constant.40.clone.1..sunk) | dynamic-update-slice | bytes 262148 | tf_op jit(solution)/shard_map/while/body/jit(dynamic_update_index_in_dim)/dynamic_update_slice | solution.py:97
  274.4 6.6 %dynamic_update_slice.29 = bf16[16,256,256]{2,0,1:T(8,128)(2,1)} dynamic-update-slice(bf16[16,256,256]{2,0,1:T(8,128)(2,1)} %get-tuple-element.385, bf16[1,256,256]{2,0,1:T(2,128)(2,1)S(1)} %copy.82, s32[]{:T(128)} %get-tuple-element.384, s32[]{:T(128)} %constant.40.clone.1..sunk, s32[]{:T(128)} %constant.40.clone.1..sunk) | dynamic-update-slice | bytes 262148 | tf_op jit(solution)/shard_map/while/body/jit(dynamic_update_index_in_dim)/dynamic_update_slice | solution.py:97
  281.3 1.1 reshape.134
  282.4 6.5 %all-to-all-start.1 = ((f32[16,1,1024]{2,1,0:T(1,128)}), f32[16,1,1024]{2,1,0:T(1,128)S(1)}, u32[]{:S(2)}, u32[]{:S(2)}) async-start(f32[16,1,1024]{2,1,0:T(1,128)} %reshape.134), calls=%async_computation.1 | async-start | bytes 131072 | tf_op jit(solution)/shard_map/all_to_all | solution.py:104
  289.6 3.6 all-to-all-done.1
  293.2 9.5 %all_to_all.45 = f32[16,1,1024]{2,1,0:T(1,128)S(1)} all-to-all(f32[16,1,1024]{2,1,0:T(1,128)S(1)} %reshape.136), channel_id=1, replica_groups=mesh['groups'=2,'seq'=16] {'seq'}, dimensions={0} | all-to-all | bytes 131072 | tf_op jit(solution)/shard_map/all_to_all | solution.py:105
  302.6 7.1 %all-to-all-start = ((bf16[1,16,256,256]{3,1,0,2:T(8,128)(2,1)}), bf16[1,16,256,256]{3,1,0,2:T(8,128)(2,1)}, u32[]{:S(2)}, u32[]{:S(2)}) async-start(bf16[1,16,256,256]{3,1,0,2:T(8,128)(2,1)} %bitcast.75), calls=%async_computation | async-start | bytes 4194304 | tf_op jit(solution)/shard_map/all_to_all | solution.py:100
  314.5 1.6 copy.56
  316.1 7.0 %mul.52 = f32[16,16,16,4,64]{4,3,2,0,1:T(4,128)} broadcast(f32[16,16,16,4]{3,2,0,1:T(8,128)S(1)} %copy.56), dimensions={0,1,2,3} | broadcast | bytes 4259840 | tf_op jit(solution)/shard_map/mul | solution.py:112
  323.1 8.6 %mul.53 = f32[16,1,16,16,256]{4,3,0,2,1:T(8,128)} reshape(f32[16,16,16,4,64]{4,3,2,0,1:T(4,128)} %mul.52) | data formatting | bytes 8388608 | tf_op jit(solution)/shard_map/mul | solution.py:112
  332.6 24.7 %all-to-all-done = bf16[1,16,256,256]{3,1,0,2:T(8,128)(2,1)} async-done(((bf16[1,16,256,256]{3,1,0,2:T(8,128)(2,1)}), bf16[1,16,256,256]{3,1,0,2:T(8,128)(2,1)}, u32[]{:S(2)}, u32[]{:S(2)}) %all-to-all-start) | async-done | bytes 2097184 | tf_op jit(solution)/shard_map/all_to_all | solution.py:100
  357.2 2.4 copy.53
  361.3 1.2 fusion.19
  (447 shorter events, 154.7 us)
Async XLA Ops:
  7.2 354.1 %copy-start = (bf16[256,512]{1,0:T(8,128)(2,1)S(1)}, bf16[256,512]{1,0:T(8,128)(2,1)}, u32[]{:S(2)}) copy-start(bf16[256,512]{1,0:T(8,128)(2,1)} %param.27) | copy-start | bytes 786436
  7.2 82.3 %all-gather.2.cloned.1.call-start = ((), (), s32[]{:S(2)}) async-start(), calls=%async_computation.3 | async-start | bytes 2228224 | tf_op jit(solution)/shard_map/all_gather | solution.py:75
  9.1 80.3 %copy-start.7 = (s32[16]{0:T(128)S(1)}, s32[16]{0:T(128)}, u32[]{:S(2)}) copy-start(s32[16]{0:T(128)} %param.20) | copy-start | bytes 196
  9.1 2.8 copy-start.5
  9.2 3.0 copy-start.3
  9.2 4.0 %copy-start.2 = (bf16[256,256]{1,0:T(8,128)(2,1)S(1)}, bf16[256,256]{1,0:T(8,128)(2,1)}, u32[]{:S(2)}) copy-start(bf16[256,256]{1,0:T(8,128)(2,1)} %get-tuple-element.371) | copy-start | bytes 393220 | tf_op jit(solution)/shard_map/while
  14.1 2.8 copy-start.5
  14.2 3.0 copy-start.3
  14.2 4.0 %copy-start.2 = (bf16[256,256]{1,0:T(8,128)(2,1)S(1)}, bf16[256,256]{1,0:T(8,128)(2,1)}, u32[]{:S(2)}) copy-start(bf16[256,256]{1,0:T(8,128)(2,1)} %get-tuple-element.371) | copy-start | bytes 393220 | tf_op jit(solution)/shard_map/while
  19.1 2.8 copy-start.5
  19.1 3.0 copy-start.3
  19.1 4.0 %copy-start.2 = (bf16[256,256]{1,0:T(8,128)(2,1)S(1)}, bf16[256,256]{1,0:T(8,128)(2,1)}, u32[]{:S(2)}) copy-start(bf16[256,256]{1,0:T(8,128)(2,1)} %get-tuple-element.371) | copy-start | bytes 393220 | tf_op jit(solution)/shard_map/while
  24.2 2.8 copy-start.5
  24.2 3.0 copy-start.3
  24.2 4.0 %copy-start.2 = (bf16[256,256]{1,0:T(8,128)(2,1)S(1)}, bf16[256,256]{1,0:T(8,128)(2,1)}, u32[]{:S(2)}) copy-start(bf16[256,256]{1,0:T(8,128)(2,1)} %get-tuple-element.371) | copy-start | bytes 393220 | tf_op jit(solution)/shard_map/while
  29.2 2.8 copy-start.5
  29.2 3.0 copy-start.3
  29.2 4.0 %copy-start.2 = (bf16[256,256]{1,0:T(8,128)(2,1)S(1)}, bf16[256,256]{1,0:T(8,128)(2,1)}, u32[]{:S(2)}) copy-start(bf16[256,256]{1,0:T(8,128)(2,1)} %get-tuple-element.371) | copy-start | bytes 393220 | tf_op jit(solution)/shard_map/while
  34.2 3.0 copy-start.3
  34.2 4.0 %copy-start.2 = (bf16[256,256]{1,0:T(8,128)(2,1)S(1)}, bf16[256,256]{1,0:T(8,128)(2,1)}, u32[]{:S(2)}) copy-start(bf16[256,256]{1,0:T(8,128)(2,1)} %get-tuple-element.371) | copy-start | bytes 393220 | tf_op jit(solution)/shard_map/while
  39.2 2.8 copy-start.5
  39.2 3.0 copy-start.3
  39.2 4.0 %copy-start.2 = (bf16[256,256]{1,0:T(8,128)(2,1)S(1)}, bf16[256,256]{1,0:T(8,128)(2,1)}, u32[]{:S(2)}) copy-start(bf16[256,256]{1,0:T(8,128)(2,1)} %get-tuple-element.371) | copy-start | bytes 393220 | tf_op jit(solution)/shard_map/while
  44.2 2.8 copy-start.5
  44.2 3.0 copy-start.3
  44.3 4.0 %copy-start.2 = (bf16[256,256]{1,0:T(8,128)(2,1)S(1)}, bf16[256,256]{1,0:T(8,128)(2,1)}, u32[]{:S(2)}) copy-start(bf16[256,256]{1,0:T(8,128)(2,1)} %get-tuple-element.371) | copy-start | bytes 393220 | tf_op jit(solution)/shard_map/while
  49.3 2.8 copy-start.5
  49.3 3.1 copy-start.3
  49.3 4.1 %copy-start.2 = (bf16[256,256]{1,0:T(8,128)(2,1)S(1)}, bf16[256,256]{1,0:T(8,128)(2,1)}, u32[]{:S(2)}) copy-start(bf16[256,256]{1,0:T(8,128)(2,1)} %get-tuple-element.371) | copy-start | bytes 393220 | tf_op jit(solution)/shard_map/while
  54.3 3.0 copy-start.3
  54.3 4.0 %copy-start.2 = (bf16[256,256]{1,0:T(8,128)(2,1)S(1)}, bf16[256,256]{1,0:T(8,128)(2,1)}, u32[]{:S(2)}) copy-start(bf16[256,256]{1,0:T(8,128)(2,1)} %get-tuple-element.371) | copy-start | bytes 393220 | tf_op jit(solution)/shard_map/while
  59.3 3.0 copy-start.3
  59.3 4.0 %copy-start.2 = (bf16[256,256]{1,0:T(8,128)(2,1)S(1)}, bf16[256,256]{1,0:T(8,128)(2,1)}, u32[]{:S(2)}) copy-start(bf16[256,256]{1,0:T(8,128)(2,1)} %get-tuple-element.371) | copy-start | bytes 393220 | tf_op jit(solution)/shard_map/while
  64.4 3.0 copy-start.3
  64.4 4.0 %copy-start.2 = (bf16[256,256]{1,0:T(8,128)(2,1)S(1)}, bf16[256,256]{1,0:T(8,128)(2,1)}, u32[]{:S(2)}) copy-start(bf16[256,256]{1,0:T(8,128)(2,1)} %get-tuple-element.371) | copy-start | bytes 393220 | tf_op jit(solution)/shard_map/while
  69.4 3.0 copy-start.3
  69.4 4.0 %copy-start.2 = (bf16[256,256]{1,0:T(8,128)(2,1)S(1)}, bf16[256,256]{1,0:T(8,128)(2,1)}, u32[]{:S(2)}) copy-start(bf16[256,256]{1,0:T(8,128)(2,1)} %get-tuple-element.371) | copy-start | bytes 393220 | tf_op jit(solution)/shard_map/while
  74.4 3.0 copy-start.3
  74.4 4.0 %copy-start.2 = (bf16[256,256]{1,0:T(8,128)(2,1)S(1)}, bf16[256,256]{1,0:T(8,128)(2,1)}, u32[]{:S(2)}) copy-start(bf16[256,256]{1,0:T(8,128)(2,1)} %get-tuple-element.371) | copy-start | bytes 393220 | tf_op jit(solution)/shard_map/while
  79.4 3.0 copy-start.3
  79.4 4.0 %copy-start.2 = (bf16[256,256]{1,0:T(8,128)(2,1)S(1)}, bf16[256,256]{1,0:T(8,128)(2,1)}, u32[]{:S(2)}) copy-start(bf16[256,256]{1,0:T(8,128)(2,1)} %get-tuple-element.371) | copy-start | bytes 393220 | tf_op jit(solution)/shard_map/while
  84.4 3.0 copy-start.3
  84.4 4.0 %copy-start.2 = (bf16[256,256]{1,0:T(8,128)(2,1)S(1)}, bf16[256,256]{1,0:T(8,128)(2,1)}, u32[]{:S(2)}) copy-start(bf16[256,256]{1,0:T(8,128)(2,1)} %get-tuple-element.371) | copy-start | bytes 393220 | tf_op jit(solution)/shard_map/while
  282.4 10.8 %all-to-all-start.1 = ((f32[16,1,1024]{2,1,0:T(1,128)}), f32[16,1,1024]{2,1,0:T(1,128)S(1)}, u32[]{:S(2)}, u32[]{:S(2)}) async-start(f32[16,1,1024]{2,1,0:T(1,128)} %reshape.134), calls=%async_computation.1 | async-start | bytes 131072 | tf_op jit(solution)/shard_map/all_to_all | solution.py:104
  302.6 7.1 %copy-start.6 = (bf16[512]{0:T(512)(128)(2,1)S(1)}, bf16[512]{0:T(512)(128)(2,1)}, u32[]{:S(2)}) copy-start(bf16[512]{0:T(512)(128)(2,1)} %param.29) | copy-start | bytes 3076
  302.6 54.6 %all-to-all-start = ((bf16[1,16,256,256]{3,1,0,2:T(8,128)(2,1)}), bf16[1,16,256,256]{3,1,0,2:T(8,128)(2,1)}, u32[]{:S(2)}, u32[]{:S(2)}) async-start(bf16[1,16,256,256]{3,1,0,2:T(8,128)(2,1)} %bitcast.75), calls=%async_computation | async-start | bytes 4194304 | tf_op jit(solution)/shard_map/all_to_all | solution.py:100
  323.1 8.6 %copy-start.4 = (f32[16,4,16]{2,1,0:T(4,128)S(1)}, f32[16,4,16]{2,1,0:T(4,128)}, u32[]{:S(2)}) copy-start(f32[16,4,16]{2,1,0:T(4,128)} %get-tuple-element.229) | copy-start | bytes 12292
  357.2 2.8 copy-start.1
  (12 other events, 26.9 us)
Sparse Core Ops, SparseCore 0:
  10.7 42.2 all-gather.1
where the time goes:
time: 374 us; the launch traced here: 369 us
  local copies, waits for them, and re-layouts  217 us (58%)
  matrix products  54.2 us (14%)
  other arithmetic  31.3 us (8%)
  waiting for transfers between devices  28.2 us (8%)
  between operations  14.2 us (4%)
  starting transfers between devices  13.6 us (4%)
  blocking collectives  9.45 us (3%)
    dynamic_update_slice x48, local copies, waits for them, and re-layouts, on_device(): lax.map(local_partials, (queries, all_keys, all_values, live_mask))  109 us
    dynamic_slice x112, local copies, waits for them, and re-layouts, on_device(): lax.map(local_partials, (queries, all_keys, all_values, live_mask))  52.3 us
    dynamic_slice x32, local copies, waits for them, and re-layouts, on_device(): all_keys, all_values = lax.map(project, (codes, scale_index))  27 us
    all_to_all x1, waiting for transfers between devices, on_device(): lax.all_to_all(numerators[None].astype(jnp.bfloat16), 'seq', split_axis=2...  24.7 us
    dot_general x16, matrix products, project(): jnp.dot(history, value_weight, preferred_element_type=jnp.float32)  15.9 us
    dot_general x16, matrix products, project(): jnp.dot(history, key_weight, preferred_element_type=jnp.float32)  15.8 us
    mul x2, local copies, waits for them, and re-layouts, on_device(): got_numerators.reshape(sources, user_count, cand_local, HEADS, head_size)  15.6 us
    reduce_sum x16, other arithmetic, local_partials(): jnp.sum(weights, axis=2)  10.1 us
  transfers between devices with their start and end apart: 3, of which 2 were waited for; matrix products, arithmetic and copies ran while one was open for 28% of the time, Pallas kernels for 0%

commit v1 on v0

v1 whole, which is shorter than its diff:
```python
import functools
import math

import jax
import jax.numpy as jnp
from jax import lax
from jax.experimental import pallas as pl
from jax.experimental.pallas import tpu as pltpu
from jax.sharding import PartitionSpec as P

HEADS = 4
MESH = pl.DeviceIdType.MESH
DEAD = -1e30
NT = (((1,), (1,)), ((), ()))


def mm(a, b, dims=(((1,), (0,)), ((), ()))):
    return lax.dot_general(a, b, dims, preferred_element_type=jnp.float32)


def kernel(
    n,
    chunk,
    lengths,
    cand,
    codes_hbm,
    index,
    table,
    wq,
    wk,
    wv,
    wo,
    gain,
    wh,
    bias,
    ws,
    interest_out,
    logits_out,
    codes,
    scales,
    wkv,
    qown,
    qall,
    kvown,
    kvsend,
    kvrecv,
    nsend,
    stats,
    nrecv,
    srecv,
    attended,
    code_sem,
    q_ssem,
    q_rsem,
    kv_ssem,
    kv_rsem,
    n_ssem,
    n_rsem,
    s_ssem,
    s_rsem,
):
    users, cl, width = cand.shape
    words = codes.shape[1]
    hist = 4 * words
    half = width // 2
    hs = width // HEADS
    rows = n * cl
    me = lax.axis_index("seq")
    core = lax.rem(me, 2)
    partner = me + 1 - 2 * core
    fetch = pltpu.make_async_copy(codes_hbm, codes, code_sem)
    fetch.start()

    def peer(i):
        return lax.rem(me + (2 * n - i - 1), n)

    barrier = pltpu.get_barrier_semaphore()
    for i in range(n - 1):
        pl.semaphore_signal(barrier, inc=1, device_id={"seq": peer(i)}, device_id_type=MESH)

    queries = (mm(cand[...].reshape(users * cl, width), wq[...])).astype(jnp.bfloat16)
    queries = (queries.astype(jnp.float32) * (1.0 / math.sqrt(hs))).astype(jnp.bfloat16)
    q3 = queries.reshape(users, cl, width)
    qown[0] = q3[:, :, :half]
    qown[1] = q3[:, :, half:]
    mine_q = jnp.where(core == 0, q3[:, :, :half].astype(jnp.float32), q3[:, :, half:].astype(jnp.float32))
    qall[:, n - 1] = mine_q.astype(jnp.bfloat16)

    pl.semaphore_wait(barrier, n - 1)

    def remote(src, dst, ssem, rsem, dev):
        return pltpu.make_async_remote_copy(
            src_ref=src, dst_ref=dst, send_sem=ssem, recv_sem=rsem,
            device_id={"seq": dev}, device_id_type=MESH,
        )

    for c in range(users // chunk):
        part = pl.ds(c * chunk, chunk)
        for i in range(n - 1):
            dev = peer(n - 2 - i)
            remote(
                qown.at[lax.rem(dev, 2), part], qall.at[part, i],
                q_ssem, q_rsem.at[c], dev,
            ).start()

    first = core == 0

    def pick(w, a):
        lo, hi = w[:, :half].astype(jnp.float32), w[:, half:].astype(jnp.float32)
        return jnp.where(a, lo, hi).astype(jnp.bfloat16)

    other = core == 1
    wkv[:, 0:half] = pick(wk[...], first)
    wkv[:, half:2 * half] = pick(wv[...], first)
    wkv[:, 2 * half:3 * half] = pick(wk[...], other)
    wkv[:, 3 * half:] = pick(wv[...], other)

    ids = index[...].reshape(users * 8, index.shape[2])
    low = lax.bitwise_and(ids, 127)
    found = jnp.zeros(ids.shape, jnp.float32)
    for g in range(table.shape[0]):
        line = jnp.broadcast_to(table[g:g + 1, :], (ids.shape[0], 128))
        got = jnp.take_along_axis(line, low, axis=1, mode="promise_in_bounds")
        found = jnp.where(lax.shift_right_logical(ids, 7) == g, got, found)
    scales[...] = found.reshape(scales.shape)
    stats[...] = jnp.zeros_like(stats)
    fetch.wait()

    lane = lax.broadcasted_iota(jnp.int32, (1, half), 1)
    head0 = lane < hs

    def project(u):
        word = codes[u]
        cols = jnp.transpose(scales[u])
        parts = []
        for k in range(4):
            code = lax.shift_right_arithmetic(lax.shift_left(word, jnp.int32(24 - 8 * k)), jnp.int32(24))
            parts.append((code.astype(jnp.float32) * cols[:, k:k + 1]).astype(jnp.bfloat16))
        history = jnp.concatenate(parts, axis=0)
        kvown[u] = mm(history, wkv[:, :width]).astype(jnp.bfloat16)
        kvsend[u] = mm(history, wkv[:, width:]).astype(jnp.bfloat16)
        remote(kvsend.at[u], kvrecv.at[u], kv_ssem.at[u], kv_rsem.at[u], partner).start()

    spot = lax.broadcasted_iota(jnp.int32, (1, hist), 1)
    spot = 4 * lax.rem(spot, words) + lax.div(spot, words)

    def attend(u):
        remote(kvsend.at[u], kvrecv.at[u], kv_ssem.at[u], kv_rsem.at[u], partner).wait()
        q = qall[u].reshape(rows, half)
        length = lengths[u]
        biases = [
            jnp.where(spot + dev * hist < length, 0.0, DEAD) for dev in (me, partner)
        ]
        outs, peaks = [], []
        for h in range(2):
            on = head0 if h == 0 else jnp.logical_not(head0)
            qh = jnp.where(on, q, jnp.zeros_like(q))
            s = [
                mm(qh, kv[u][:, :half], NT) + b
                for kv, b in zip((kvown, kvrecv), biases)
            ]
            peak = jnp.max(jnp.maximum(s[0], s[1]), axis=1, keepdims=True)
            acc = None
            for kv, x in zip((kvown, kvrecv), s):
                v = kv[u][:, half:]
                v = jnp.where(on, v, jnp.ones_like(v))
                o = mm(jnp.exp(x - peak).astype(jnp.bfloat16), v)
                acc = o if acc is None else acc + o
            outs.append(acc)
            peaks.append(peak)
        nsend[u] = jnp.where(head0, outs[0], outs[1]).astype(jnp.bfloat16).reshape(n, cl, half)
        values = (peaks[0], peaks[1], outs[0][:, hs:hs + 1], outs[1][:, 0:1])
        st = stats[...].reshape(rows, 128)
        wide = lax.broadcasted_iota(jnp.int32, (1, 128), 1)
        for r in range(4):
            st = jnp.where(wide == 4 * u + r, values[r], st)
        stats[...] = st.reshape(stats.shape)
        for i in range(n - 1):
            remote(nsend.at[u, i], nrecv.at[i, u], n_ssem, n_rsem, peer(i)).start()
        nrecv[n - 1, u] = nsend[u, n - 1]

    project(0)

    def group(c, carry):
        landed = qall.at[pl.ds(c * chunk, chunk), pl.ds(0, n - 1)]
        remote(landed, landed, q_ssem, q_rsem.at[c], partner).wait_recv()

        def body(k, carry):
            u = c * chunk + k

            @pl.when(u + 1 < users)
            def _():
                project(u + 1)

            attend(u)
            return carry

        return lax.fori_loop(0, chunk, body, carry)

    lax.fori_loop(0, users // chunk, group, 0)

    for i in range(n - 1):
        remote(stats.at[i], srecv.at[i], s_ssem, s_rsem, peer(i)).start()
    srecv[n - 1] = stats[n - 1]
    qdone = qall.at[:, pl.ds(0, n - 1)]
    remote(qdone, qdone, q_ssem, q_rsem.at[0], partner).wait_send()
    sdone = srecv.at[pl.ds(0, n - 1)]
    remote(sdone, sdone, s_ssem, s_rsem, partner).wait()
    ndone = nrecv.at[pl.ds(0, n - 1)]
    remote(ndone, ndone, n_ssem, n_rsem, partner).wait()

    shares = [None] * n
    for parity in range(2):
        slots = range(parity, n, 2)
        top = functools.reduce(jnp.maximum, [srecv[i] for i in slots])
        factors = [jnp.exp(srecv[i] - top) for i in slots]
        sums = [f * pltpu.roll(srecv[i], 126, axis=1) for f, i in zip(factors, slots)]
        total = functools.reduce(jnp.add, sums)
        for f, i in zip(factors, slots):
            shares[i] = f / total
    share = jnp.concatenate(shares, axis=0)
    stats[...] = share.reshape(stats.shape)

    def merge(u, carry):
        turned = pltpu.roll(stats[...].reshape(rows, 128), lax.rem(128 - 4 * u, 128), axis=1)
        scale = jnp.where(head0, turned[:, 0:1], turned[:, 1:2])
        part = nrecv[:, u].astype(jnp.float32) * scale.reshape(n, cl, half)
        same = functools.reduce(jnp.add, [part[i] for i in range(1, n, 2)])
        cross = functools.reduce(jnp.add, [part[i] for i in range(0, n, 2)])
        attended[u, :, :half] = jnp.where(first, same, cross).astype(jnp.bfloat16)
        attended[u, :, half:] = jnp.where(first, cross, same).astype(jnp.bfloat16)
        return carry

    lax.fori_loop(0, users, merge, 0)

    interest = mm(attended[...].reshape(users * cl, width), wo[...]).astype(jnp.bfloat16)
    interest_out[...] = interest.reshape(users, cl, width)
    floats = interest.astype(jnp.float32)
    spread = jnp.mean(floats * floats, axis=1, keepdims=True)
    normed = (floats * lax.rsqrt(spread + 1e-06) * gain[...]).astype(jnp.bfloat16)
    v = mm(normed, wh[...]) + bias[...]
    hidden = (v / (1.0 + jnp.exp(-v))).astype(jnp.bfloat16)
    logits_out[...] = mm(jnp.broadcast_to(ws[...], (16, ws.shape[1])), hidden, NT)[0:1]


def on_device(
    n,
    candidates,
    codes,
    scale_index,
    lengths,
    scale_table,
    query_weight,
    key_weight,
    value_weight,
    out_weight,
    norm_gain,
    hidden_weight,
    hidden_bias,
    score_weight,
):
    users, cl, width = candidates.shape
    words = codes.shape[1]
    half = width // 2
    chunk = math.gcd(users, 4)
    index = jnp.transpose(scale_index.reshape(users, words, 4), (0, 2, 1))
    index = jnp.pad(index, ((0, 0), (0, 4), (0, 0)))
    vmem = pl.BlockSpec(memory_space=pltpu.VMEM)
    interest, logits = pl.pallas_call(
        functools.partial(kernel, n, chunk),
        out_shape=(
            jax.ShapeDtypeStruct((users, cl, width), jnp.bfloat16),
            jax.ShapeDtypeStruct((1, users * cl), jnp.float32),
        ),
        in_specs=[pl.BlockSpec(memory_space=pltpu.SMEM), vmem, pl.BlockSpec(memory_space=pl.ANY)] + [vmem] * 10,
        out_specs=(vmem, vmem),
        scratch_shapes=[
            pltpu.VMEM((users, words, width), jnp.int32),
            pltpu.VMEM((users, 8, words), jnp.float32),
            pltpu.VMEM((width, 2 * width), jnp.bfloat16),
            pltpu.VMEM((2, users, cl, half), jnp.bfloat16),
            pltpu.VMEM((users, n, cl, half), jnp.bfloat16),
            pltpu.VMEM((users, 4 * words, width), jnp.bfloat16),
            pltpu.VMEM((users, 4 * words, width), jnp.bfloat16),
            pltpu.VMEM((users, 4 * words, width), jnp.bfloat16),
            pltpu.VMEM((users, n, cl, half), jnp.bfloat16),
            pltpu.VMEM((n, cl, 128), jnp.float32),
            pltpu.VMEM((n, users, cl, half), jnp.bfloat16),
            pltpu.VMEM((n, cl, 128), jnp.float32),
            pltpu.VMEM((users, cl, width), jnp.bfloat16),
            pltpu.SemaphoreType.DMA,
            pltpu.SemaphoreType.DMA,
            pltpu.SemaphoreType.DMA((users // chunk,)),
            pltpu.SemaphoreType.DMA((users,)),
            pltpu.SemaphoreType.DMA((users,)),
            pltpu.SemaphoreType.DMA,
            pltpu.SemaphoreType.DMA,
            pltpu.SemaphoreType.DMA,
            pltpu.SemaphoreType.DMA,
        ],
        compiler_params=pltpu.CompilerParams(
            collective_id=0, has_side_effects=True, vmem_limit_bytes=60 * 1024 * 1024
        ),
    )(
        lengths,
        candidates,
        codes,
        index,
        scale_table.reshape(-1, 128),
        query_weight,
        key_weight,
        value_weight,
        out_weight,
        norm_gain.reshape(1, -1),
        hidden_weight,
        hidden_bias.reshape(1, -1),
        score_weight.reshape(1, -1),
    )
    return interest, logits.reshape(users, cl)


def solution(mesh):
    placed = (
        P("groups", "seq", None),
        P("groups", "seq", None),
        P("groups", "seq"),
        P("groups"),
    ) + (P(),) * 9
    return jax.shard_map(
        functools.partial(on_device, mesh.shape["seq"]),
        mesh=mesh,
        in_specs=placed,
        out_specs=(P("groups", "seq", None), P("groups", "seq")),
        check_vma=False,
    )
```

time: 374 us -> 69.8 us (0.19)
  the two profiles are of different devices: /device:TPU:13 before, /device:TPU:0 now
where the time goes in v1:
time: 69.8 us; the launch traced here: 69.5 us
  Pallas kernels  61.9 us (89%)
  local copies, waits for them, and re-layouts  5.66 us (8%)
  other arithmetic  1.32 us (2%)
    pallas_call x1, Pallas kernels, on_device(): pl.pallas_call(functools.partial(kernel, n, chunk), out_shape=(jax.ShapeD...  61.9 us
    unnamed x2, local copies, waits for them, and re-layouts  2.45 us

profile of v1, /device:TPU:0, one launch (start us, length us, event | category | flops | bytes accessed | tf_op | source)
XLA Modules:
  0.0 69.5 jit_solution(18222284130268446351)
XLA Ops:
  0.6 0.9 %copy.15 = s32[16,512]{0,1:T(8,128)S(1)} copy(s32[16,512]{1,0:T(8,128)} %param.15) | data formatting | bytes 65536 | tf_op args[2]
  1.5 0.1 copy.16
  1.6 0.7 pad.4.index
  2.3 1.3 %reshape.26.ws = bf16[1,512]{1,0:T(2,128)(2,1)} reshape(bf16[512]{0:T(512)(128)(2,1)} %param.25) | data formatting | bytes 2048 | tf_op jit(solution)/shard_map/reshape | solution.py:317
  3.5 61.9 %shard_map.140 = (bf16[16,16,256]{2,1,0:T(8,128)(2,1)}, f32[1,256]{1,0:T(1,128)}) custom-call(s32[16]{0:T(128)} %lengths.1, bf16[16,16,256]{2,1,0:T(8,128)(2,1)} %cand.1, s32[16,128,256]{2,1,0:T(8,128)} %codes_hbm.1, s32[16,8,128]{2,1,0:T(8,128)} %pad.4.index, f32[2,128]{1,0:T(2,128)} %bitcast.8, bf16[256,256]{1,0:T(8,128)(2,1)} %wq.1, bf16[256,256]{1,0:T(8,128)(2,1)} %wk.1, ...), custom_call_target="tpu_custom_call" | custom-call | tf_op jit(solution)/shard_map/pallas_call | solution.py:269
  65.4 0.5 broadcast.5
  65.9 1.3 %reduce.3 = f32[256]{0:T(256)S(1)} reduce(f32[1,256]{1,0:T(1,128)} %get-tuple-element.5, f32[]{:T(128)} %broadcast.5), dimensions={0}, to_apply=%get-tuple-element.5.reduce_sub_computation.3 | reduce | bytes 2052 | tf_op jit(solution)/shard_map/pallas_call | solution.py:269
  67.3 0.7 reshape.27
  68.0 1.6 %copy.18 = bf16[16,16,256]{2,1,0:T(8,128)(2,1)} copy(bf16[16,16,256]{2,1,0:T(8,128)(2,1)} %get-tuple-element.8) | data formatting | bytes 262144

commit v2 on v1

--- a/solution.py
+++ b/solution.py
@@ -52,6 +52,8 @@
     code_sem,
     q_ssem,
     q_rsem,
+    f_ssem,
+    f_rsem,
     kv_ssem,
     kv_rsem,
     n_ssem,
@@ -71,11 +73,18 @@
     fetch = pltpu.make_async_copy(codes_hbm, codes, code_sem)
     fetch.start()
 
+    near = n // 2
+
     def peer(i):
-        return lax.rem(me + (2 * n - i - 1), n)
+        there = me
+        for bit in range(n.bit_length() - 1):
+            place = 0 if bit == 0 else bit - 1 if bit > 1 else n.bit_length() - 2
+            if (i >> place) & 1:
+                there = there + (1 << bit) * (1 - 2 * lax.rem(lax.div(me, 1 << bit), 2))
+        return there
 
     barrier = pltpu.get_barrier_semaphore()
-    for i in range(n - 1):
+    for i in range(1, n):
         pl.semaphore_signal(barrier, inc=1, device_id={"seq": peer(i)}, device_id_type=MESH)
 
     queries = (mm(cand[...].reshape(users * cl, width), wq[...])).astype(jnp.bfloat16)
@@ -84,7 +93,7 @@
     qown[0] = q3[:, :, :half]
     qown[1] = q3[:, :, half:]
     mine_q = jnp.where(core == 0, q3[:, :, :half].astype(jnp.float32), q3[:, :, half:].astype(jnp.float32))
-    qall[:, n - 1] = mine_q.astype(jnp.bfloat16)
+    qall[:, 0] = mine_q.astype(jnp.bfloat16)
 
     pl.semaphore_wait(barrier, n - 1)
 
@@ -96,12 +105,12 @@
 
     for c in range(users // chunk):
         part = pl.ds(c * chunk, chunk)
-        for i in range(n - 1):
-            dev = peer(n - 2 - i)
+        for i in range(1, near):
+            dev = peer(i)
             remote(
-                qown.at[lax.rem(dev, 2), part], qall.at[part, i],
-                q_ssem, q_rsem.at[c], dev,
+                qown.at[lax.rem(dev, 2), part], qall.at[part, i], q_ssem, q_rsem.at[c], dev
             ).start()
+        remote(qall.at[part, 0], qall.at[part, near], f_ssem, f_rsem.at[c], peer(near)).start()
 
     first = core == 0
 
@@ -115,14 +124,24 @@
     wkv[:, 2 * half:3 * half] = pick(wk[...], other)
     wkv[:, 3 * half:] = pick(wv[...], other)
 
-    ids = index[...].reshape(users * 8, index.shape[2])
-    low = lax.bitwise_and(ids, 127)
-    found = jnp.zeros(ids.shape, jnp.float32)
-    for g in range(table.shape[0]):
-        line = jnp.broadcast_to(table[g:g + 1, :], (ids.shape[0], 128))
-        got = jnp.take_along_axis(line, low, axis=1, mode="promise_in_bounds")
-        found = jnp.where(lax.shift_right_logical(ids, 7) == g, got, found)
-    scales[...] = found.reshape(scales.shape)
+    place = lax.broadcasted_iota(jnp.int32, (users, 128), 1)
+
+    def lookup(line, at):
+        return jnp.take_along_axis(line, at, axis=1, mode="promise_in_bounds")
+
+    for block in range(words // 128):
+        for k in range(4):
+            ids = jnp.zeros((users, 128), jnp.int32)
+            for j in range(4):
+                start = 512 * block + 128 * j
+                got = lookup(index[:, start:start + 128], 4 * lax.rem(place, 32) + k)
+                ids = jnp.where(lax.div(place, 32) == j, got, ids)
+            found = jnp.zeros((users, 128), jnp.float32)
+            for g in range(table.shape[0]):
+                line = jnp.broadcast_to(table[g:g + 1, :], (users, 128))
+                got = lookup(line, lax.bitwise_and(ids, 127))
+                found = jnp.where(lax.shift_right_logical(ids, 7) == g, got, found)
+            scales[:, k, 128 * block:128 * block + 128] = found
     stats[...] = jnp.zeros_like(stats)
     fetch.wait()
 
@@ -175,15 +194,27 @@
         for r in range(4):
             st = jnp.where(wide == 4 * u + r, values[r], st)
         stats[...] = st.reshape(stats.shape)
-        for i in range(n - 1):
+        for i in range(1, n):
             remote(nsend.at[u, i], nrecv.at[i, u], n_ssem, n_rsem, peer(i)).start()
-        nrecv[n - 1, u] = nsend[u, n - 1]
-
+        nrecv[0, u] = nsend[u, 0]
+
+    def forward(c):
+        landed = qall.at[pl.ds(c * chunk, chunk), pl.ds(1, near - 1)]
+        remote(landed, landed, q_ssem, q_rsem.at[c], partner).wait_recv()
+        target = qall.at[pl.ds(c * chunk, chunk), pl.ds(near + 1, near - 1)]
+        remote(landed, target, f_ssem, f_rsem.at[c], peer(near)).start()
+
+    groups = users // chunk
     project(0)
+    forward(0)
 
     def group(c, carry):
-        landed = qall.at[pl.ds(c * chunk, chunk), pl.ds(0, n - 1)]
-        remote(landed, landed, q_ssem, q_rsem.at[c], partner).wait_recv()
+        @pl.when(c + 1 < groups)
+        def _():
+            forward(c + 1)
+
+        landed = qall.at[pl.ds(c * chunk, chunk), pl.ds(near, near)]
+        remote(landed, landed, f_ssem, f_rsem.at[c], partner).wait_recv()
 
         def body(k, carry):
             u = c * chunk + k
@@ -197,16 +228,18 @@
 
         return lax.fori_loop(0, chunk, body, carry)
 
-    lax.fori_loop(0, users // chunk, group, 0)
-
-    for i in range(n - 1):
+    lax.fori_loop(0, groups, group, 0)
+
+    for i in range(1, n):
         remote(stats.at[i], srecv.at[i], s_ssem, s_rsem, peer(i)).start()
-    srecv[n - 1] = stats[n - 1]
-    qdone = qall.at[:, pl.ds(0, n - 1)]
+    srecv[0] = stats[0]
+    qdone = qall.at[:, pl.ds(1, near - 1)]
     remote(qdone, qdone, q_ssem, q_rsem.at[0], partner).wait_send()
-    sdone = srecv.at[pl.ds(0, n - 1)]
+    fdone = qall.at[:, pl.ds(near, near)]
+    remote(fdone, fdone, f_ssem, f_rsem.at[0], partner).wait_send()
+    sdone = srecv.at[pl.ds(1, n - 1)]
     remote(sdone, sdone, s_ssem, s_rsem, partner).wait()
-    ndone = nrecv.at[pl.ds(0, n - 1)]
+    ndone = nrecv.at[pl.ds(1, n - 1)]
     remote(ndone, ndone, n_ssem, n_rsem, partner).wait()
 
     shares = [None] * n
@@ -219,14 +252,21 @@
         for f, i in zip(factors, slots):
             shares[i] = f / total
     share = jnp.concatenate(shares, axis=0)
-    stats[...] = share.reshape(stats.shape)
+    wide = lax.broadcasted_iota(jnp.int32, (1, 128), 1)
+    used = jnp.logical_and(lax.rem(wide, 4) < 2, wide < 4 * users)
+    share = jnp.where(used, share, 0.0)
+    high = share.astype(jnp.bfloat16)
+    low = (share - high.astype(jnp.float32)).astype(jnp.bfloat16)
+    share = jnp.concatenate([high, low], axis=1)
+    source = lax.rem(lax.broadcasted_iota(jnp.int32, (256, half), 0), 128)
+    target = lax.div(lax.broadcasted_iota(jnp.int32, (256, half), 1), hs)
 
     def merge(u, carry):
-        turned = pltpu.roll(stats[...].reshape(rows, 128), lax.rem(128 - 4 * u, 128), axis=1)
-        scale = jnp.where(head0, turned[:, 0:1], turned[:, 1:2])
+        spread = jnp.where(source == 4 * u + target, 1.0, 0.0).astype(jnp.bfloat16)
+        scale = mm(share, spread)
         part = nrecv[:, u].astype(jnp.float32) * scale.reshape(n, cl, half)
-        same = functools.reduce(jnp.add, [part[i] for i in range(1, n, 2)])
-        cross = functools.reduce(jnp.add, [part[i] for i in range(0, n, 2)])
+        same = functools.reduce(jnp.add, [part[i] for i in range(0, n, 2)])
+        cross = functools.reduce(jnp.add, [part[i] for i in range(1, n, 2)])
         attended[u, :, :half] = jnp.where(first, same, cross).astype(jnp.bfloat16)
         attended[u, :, half:] = jnp.where(first, cross, same).astype(jnp.bfloat16)
         return carry
@@ -240,7 +280,16 @@
     normed = (floats * lax.rsqrt(spread + 1e-06) * gain[...]).astype(jnp.bfloat16)
     v = mm(normed, wh[...]) + bias[...]
     hidden = (v / (1.0 + jnp.exp(-v))).astype(jnp.bfloat16)
-    logits_out[...] = mm(jnp.broadcast_to(ws[...], (16, ws.shape[1])), hidden, NT)[0:1]
+    line = mm(jnp.broadcast_to(ws[...].astype(jnp.float32).reshape(1, -1), (16, ws.shape[0])).astype(jnp.bfloat16), hidden, NT)[0:1]
+    row = lax.broadcasted_iota(jnp.int32, (users, users * cl), 0)
+    column = lax.broadcasted_iota(jnp.int32, (users, users * cl), 1)
+    spread = jnp.where(lax.div(column, cl) == row, line, 0.0)
+    chosen = lax.rem(lax.broadcasted_iota(jnp.int32, (users * cl, cl), 0), cl)
+    chosen = (chosen == lax.broadcasted_iota(jnp.int32, (users * cl, cl), 1)).astype(jnp.float32)
+    logits_out[...] = lax.dot_general(
+        spread, chosen, (((1,), (0,)), ((), ())),
+        precision=lax.Precision.HIGHEST, preferred_element_type=jnp.float32,
+    )
 
 
 def on_device(
@@ -262,15 +311,13 @@
     users, cl, width = candidates.shape
     words = codes.shape[1]
     half = width // 2
-    chunk = math.gcd(users, 4)
-    index = jnp.transpose(scale_index.reshape(users, words, 4), (0, 2, 1))
-    index = jnp.pad(index, ((0, 0), (0, 4), (0, 0)))
+    chunk = math.gcd(users, 2)
     vmem = pl.BlockSpec(memory_space=pltpu.VMEM)
-    interest, logits = pl.pallas_call(
+    return pl.pallas_call(
         functools.partial(kernel, n, chunk),
         out_shape=(
             jax.ShapeDtypeStruct((users, cl, width), jnp.bfloat16),
-            jax.ShapeDtypeStruct((1, users * cl), jnp.float32),
+            jax.ShapeDtypeStruct((users, cl), jnp.float32),
         ),
         in_specs=[pl.BlockSpec(memory_space=pltpu.SMEM), vmem, pl.BlockSpec(memory_space=pl.ANY)] + [vmem] * 10,
         out_specs=(vmem, vmem),
@@ -291,6 +338,8 @@
             pltpu.SemaphoreType.DMA,
             pltpu.SemaphoreType.DMA,
             pltpu.SemaphoreType.DMA((users // chunk,)),
+            pltpu.SemaphoreType.DMA,
+            pltpu.SemaphoreType.DMA((users // chunk,)),
             pltpu.SemaphoreType.DMA((users,)),
             pltpu.SemaphoreType.DMA((users,)),
             pltpu.SemaphoreType.DMA,
@@ -305,7 +354,7 @@
         lengths,
         candidates,
         codes,
-        index,
+        scale_index,
         scale_table.reshape(-1, 128),
         query_weight,
         key_weight,
@@ -314,9 +363,8 @@
         norm_gain.reshape(1, -1),
         hidden_weight,
         hidden_bias.reshape(1, -1),
-        score_weight.reshape(1, -1),
+        score_weight,
     )
-    return interest, logits.reshape(users, cl)
 
 
 def solution(mesh):

time: 69.8 us -> 58.9 us (0.84)
  Pallas kernels: 61.9 us -> 55.1 us
  local copies, waits for them, and re-layouts: 5.66 us -> 2.86 us
  other arithmetic: 1.32 us -> 0 us
    pallas_call x1, Pallas kernels: 61.9 us -> 55.1 us  [on_device(): pl.pallas_call(functools.partial(kernel, n, chunk), out_shape=(jax.ShapeD...]
    reshape x3 -> x0, local copies, waits for them, and re-layouts: 2.04 us -> none  [the longest x1 1.26 us: on_device(): score_weight.reshape(1, -1)]
    pallas_call x1 -> x0, other arithmetic: 1.32 us -> none  [on_device(): pl.pallas_call(functools.partial(kernel, n, chunk), out_shape=(jax.ShapeD...]
where the time goes in v2:
time: 58.9 us; the launch traced here: 58.6 us
  Pallas kernels  55.1 us (94%)
  local copies, waits for them, and re-layouts  2.86 us (5%)
  between operations  0.64 us (1%)
    pallas_call x1, Pallas kernels, on_device(): pl.pallas_call(functools.partial(kernel, n, chunk), out_shape=(jax.ShapeD...  55.1 us
    unnamed x2, local copies, waits for them, and re-layouts  2.86 us

profile of v2, /device:TPU:0, one launch (start us, length us, event | category | flops | bytes accessed | tf_op | source)
XLA Modules:
  0.0 58.6 jit_solution(18076561928603916523)
XLA Ops:
  0.6 55.1 %shard_map.140 = (bf16[16,16,256]{2,1,0:T(8,128)(2,1)}, f32[16,16]{1,0:T(8,128)}) custom-call(s32[16]{0:T(128)} %lengths.1, bf16[16,16,256]{2,1,0:T(8,128)(2,1)} %cand.1, s32[16,128,256]{2,1,0:T(8,128)} %codes_hbm.1, s32[16,512]{1,0:T(8,128)} %index.1, f32[2,128]{1,0:T(2,128)} %bitcast.4, bf16[256,256]{1,0:T(8,128)(2,1)} %wq.1, bf16[256,256]{1,0:T(8,128)(2,1)} %wk.1, ...), custom_call_target="tpu_custom_call" | custom-call | tf_op jit(solution)/shard_map/pallas_call | solution.py:316
  55.8 1.6 %copy.17 = bf16[16,16,256]{2,1,0:T(8,128)(2,1)} copy(bf16[16,16,256]{2,1,0:T(8,128)(2,1)} %get-tuple-element.4) | data formatting | bytes 262144
  57.4 1.3 %copy.18 = f32[16,16]{1,0:T(8,128)} copy(f32[16,16]{1,0:T(8,128)} %get-tuple-element.5) | data formatting | bytes 2048
